TPU v7x, 32 devices: a whole 2x2x4 slice. The times are simulated.
32 devices in a mesh: py: 2 (over y), px: 4 (over x, core), pz: 4 (over z).
Axes of the slice: x: 2, y: 2, z: 4, core: 2. Of those that a mesh axis runs over, the one named last changes fastest.
Arguments:
- tracer: float32 [32, 512, 32, 128], P('py', 'px', 'pz'), may hold values from 0.2 to 1.8
- conductance: float32 [32, 512, 32, 128], P('py', 'px', 'pz'), may hold values from 0.03 to 0.15
- source: float32 [32, 512, 32, 128], P('py', 'px', 'pz'), may hold values from -0.2 to 0.2
Outputs:
- potential: float32 [32, 512, 32, 128], P('py', 'px', 'pz')
- tracer_end: float32 [32, 512, 32, 128], P('py', 'px', 'pz')
All inputs are finite; a program needn't handle non-finite values.
Results may differ from a plain program's by a relative error of at most 0.00002.
Values sent between devices are 32-bit elements; how exact they have to be, the bound alone decides.
A program may use at most 320 MiB of HBM per device.

v0:
```python
import jax
import jax.numpy as jnp
from jax import lax
from jax.sharding import PartitionSpec as P

STEPS = 4


def padded_2(block, sides, width):
    for axis, dim in sides:
        count = lax.axis_size(axis)
        forward = [(i, i + 1) for i in range(count - 1)]
        forward.append((count - 1, 0))
        backward = [(target, source) for source, target in forward]
        low = lax.ppermute(
            lax.slice_in_dim(block, block.shape[dim] - width, None, axis=dim), axis, forward
        )
        high = lax.ppermute(lax.slice_in_dim(block, 0, width, axis=dim), axis, backward)
        block = jnp.concatenate([low, block, high], axis=dim)
    return block


def entering(value, axis, join, neutral):
    count, mine = (lax.axis_size(axis), lax.axis_index(axis))
    pieces = lax.all_gather(value, axis)
    so_far = jnp.full_like(value, 0) + jnp.asarray(neutral, value.dtype)

    def hop(position, so_far):
        longer = join(so_far, pieces[position])
        return jnp.where(position < mine, longer, so_far)

    return lax.fori_loop(0, count - 1, hop, so_far)


def strip_edges(values, dims):
    for dim in dims:
        values = lax.slice_in_dim(values, 1, values.shape[dim] - 1, axis=dim)
    return values


def neighbour(values, dim, start, dims):
    others = [other for other in dims if other != dim]
    values = strip_edges(values, others)
    return lax.slice_in_dim(values, start, start + values.shape[dim] - 2, axis=dim)


def one_step(padded, conductance, source):
    middle = strip_edges(padded, (0, 1, 2))
    lower = [neighbour(padded, dim, 0, (0, 1, 2)) for dim in (0, 1, 2)]
    upper = [neighbour(padded, dim, 2, (0, 1, 2)) for dim in (0, 1, 2)]
    spread = lower[0] + upper[0] + lower[1] + upper[1] + lower[2] + upper[2] - 6.0 * middle
    return middle + conductance * spread + source


def on_device(tracer, conductance, source):
    for step in range(STEPS):
        padded = padded_2(tracer, (("py", 0), ("px", 1), ("pz", 2)), 1)
        tracer = one_step(padded, conductance, source)
    here = jnp.cumsum(tracer, axis=2)
    total = lax.slice_in_dim(here, here.shape[2] - 1, here.shape[2], axis=2)

    def add_pair(earlier_total, later_total):
        return earlier_total + later_total

    below = entering(total, "pz", add_pair, jnp.zeros_like(total))
    potential = (here + below) / (tracer.shape[2] * lax.axis_size("pz"))
    return (potential, tracer)


def solution(mesh):
    placed = (P("py", "px", "pz", None), P("py", "px", "pz", None), P("py", "px", "pz", None))
    return jax.shard_map(
        on_device,
        mesh=mesh,
        in_specs=placed,
        out_specs=(P("py", "px", "pz", None), P("py", "px", "pz", None)),
        check_vma=False,
    )
```

profile of v0, /device:TPU:24, one launch (start us, length us, event | category | flops | bytes accessed | tf_op | source)
XLA Modules:
  0.0 1169.5 jit_solution(1236503037858312687)
XLA Ops:
  10.6 12.8 %collective-permute-done = f32[1,128,8,128]{3,2,1,0:T(8,128)S(1)} collective-permute-done((f32[1,128,8,128]{3,2,1,0:T(8,128)S(1)}, f32[1,128,8,128]{3,2,1,0:T(8,128)S(1)}, u32[]{:S(2)}, u32[]{:S(2)}) %collective-permute-start) | collective-permute-done | bytes 524320 | tf_op jit(solution)/shard_map/ppermute | solution.py:15
  27.4 6.0 collective-permute-done.1
  43.3 27.7 %collective-permute-done.5 = f32[18,130,1,128]{3,1,2,0:T(8,128)S(1)} collective-permute-done((f32[18,130,1,128]{3,1,2,0:T(8,128)S(1)}, f32[18,130,1,128]{3,1,2,0:T(8,128)S(1)}, u32[]{:S(2)}, u32[]{:S(2)}) %collective-permute-start.5) | collective-permute-done | bytes 1198112 | tf_op jit(solution)/shard_map/ppermute | solution.py:18
  72.3 24.6 %collective-permute-done.4 = f32[18,130,1,128]{3,1,2,0:T(8,128)S(1)} collective-permute-done((f32[18,130,1,128]{3,1,2,0:T(8,128)S(1)}, f32[18,130,1,128]{3,1,2,0:T(8,128)S(1)}, u32[]{:S(2)}, u32[]{:S(2)}) %collective-permute-start.4) | collective-permute-done | bytes 1198112 | tf_op jit(solution)/shard_map/ppermute | solution.py:15
  98.1 26.9 %fusion.31 = f32[16,128,8,128]{3,2,1,0:T(8,128)S(1)} fusion(f32[16,128,8,128]{3,2,1,0:T(8,128)} %param.7, f32[16,128,8,128]{3,2,1,0:T(8,128)} %param.5, f32[16,128,8,128]{3,2,1,0:T(8,128)} %param.6, f32[18,130,1,128]{3,2,1,0:T(1,128)S(1)} %copy.27, f32[18,1,8,128]{3,2,1,0:T(8,128)S(1)} %collective-permute-done.3, f32[18,128,8,128]{3,2,1,0:T(8,128)} %copy-done.2, ...), kind=kLoop, calls=%fused_computation.89 | loop fusion | flops 41943040 | bytes 46583808 | tf_op jit(solution)/shard_map/add | solution.py:52
  127.2 12.8 %collective-permute-done.6 = f32[1,128,8,128]{3,2,1,0:T(8,128)S(1)} collective-permute-done((f32[1,128,8,128]{3,2,1,0:T(8,128)S(1)}, f32[1,128,8,128]{3,2,1,0:T(8,128)S(1)}, u32[]{:S(2)}, u32[]{:S(2)}) %collective-permute-start.6) | collective-permute-done | bytes 524320 | tf_op jit(solution)/shard_map/ppermute | solution.py:15
  139.9 10.4 collective-permute-done.7
  161.4 28.1 %collective-permute-done.11 = f32[18,130,1,128]{3,1,2,0:T(8,128)S(1)} collective-permute-done((f32[18,130,1,128]{3,1,2,0:T(8,128)S(1)}, f32[18,130,1,128]{3,1,2,0:T(8,128)S(1)}, u32[]{:S(2)}, u32[]{:S(2)}) %collective-permute-start.11) | collective-permute-done | bytes 1198112 | tf_op jit(solution)/shard_map/ppermute | solution.py:18
  190.7 24.4 %collective-permute-done.10 = f32[18,130,1,128]{3,1,2,0:T(8,128)S(1)} collective-permute-done((f32[18,130,1,128]{3,1,2,0:T(8,128)S(1)}, f32[18,130,1,128]{3,1,2,0:T(8,128)S(1)}, u32[]{:S(2)}, u32[]{:S(2)}) %collective-permute-start.10) | collective-permute-done | bytes 1198112 | tf_op jit(solution)/shard_map/ppermute | solution.py:15
  217.4 13.7 %fusion.22 = f32[16,128,8,128]{3,2,1,0:T(8,128)} fusion(f32[16,128,8,128]{3,2,1,0:T(8,128)} %param.7, f32[16,128,8,128]{3,2,1,0:T(8,128)S(1)} %fusion.31, f32[16,128,8,128]{3,2,1,0:T(8,128)} %param.6, f32[18,130,1,128]{3,2,1,0:T(1,128)S(1)} %copy.31, f32[18,1,8,128]{3,2,1,0:T(8,128)S(1)} %collective-permute-done.9, ...), kind=kLoop, calls=%fused_computation.62 | loop fusion | flops 58720256 | bytes 37146624 | tf_op jit(solution)/shard_map/add | solution.py:52
  234.6 12.8 %collective-permute-done.12 = f32[1,128,8,128]{3,2,1,0:T(8,128)S(1)} collective-permute-done((f32[1,128,8,128]{3,2,1,0:T(8,128)S(1)}, f32[1,128,8,128]{3,2,1,0:T(8,128)S(1)}, u32[]{:S(2)}, u32[]{:S(2)}) %collective-permute-start.12) | collective-permute-done | bytes 524320 | tf_op jit(solution)/shard_map/ppermute | solution.py:15
  247.4 10.4 collective-permute-done.13
  269.6 28.0 %collective-permute-done.17 = f32[18,130,1,128]{3,1,2,0:T(8,128)S(1)} collective-permute-done((f32[18,130,1,128]{3,1,2,0:T(8,128)S(1)}, f32[18,130,1,128]{3,1,2,0:T(8,128)S(1)}, u32[]{:S(2)}, u32[]{:S(2)}) %collective-permute-start.17) | collective-permute-done | bytes 1198112 | tf_op jit(solution)/shard_map/ppermute | solution.py:18
  298.8 25.4 %collective-permute-done.16 = f32[18,130,1,128]{3,1,2,0:T(8,128)S(1)} collective-permute-done((f32[18,130,1,128]{3,1,2,0:T(8,128)S(1)}, f32[18,130,1,128]{3,1,2,0:T(8,128)S(1)}, u32[]{:S(2)}, u32[]{:S(2)}) %collective-permute-start.16) | collective-permute-done | bytes 1198112 | tf_op jit(solution)/shard_map/ppermute | solution.py:15
  326.5 13.7 %fusion.13 = f32[16,128,8,128]{3,2,1,0:T(8,128)} fusion(f32[16,128,8,128]{3,2,1,0:T(8,128)} %param.7, f32[16,128,8,128]{3,2,1,0:T(8,128)S(1)} %copy-done, f32[16,128,8,128]{3,2,1,0:T(8,128)} %param.6, f32[18,130,1,128]{3,2,1,0:T(1,128)S(1)} %copy.35, f32[18,1,8,128]{3,2,1,0:T(8,128)S(1)} %collective-permute-done.15, ...), kind=kLoop, calls=%fused_computation.35 | loop fusion | flops 58720256 | bytes 37146624 | tf_op jit(solution)/shard_map/add | solution.py:52
  343.8 12.8 %collective-permute-done.18 = f32[1,128,8,128]{3,2,1,0:T(8,128)S(1)} collective-permute-done((f32[1,128,8,128]{3,2,1,0:T(8,128)S(1)}, f32[1,128,8,128]{3,2,1,0:T(8,128)S(1)}, u32[]{:S(2)}, u32[]{:S(2)}) %collective-permute-start.18) | collective-permute-done | bytes 524320 | tf_op jit(solution)/shard_map/ppermute | solution.py:15
  356.5 10.1 collective-permute-done.19
  378.5 27.9 %collective-permute-done.23 = f32[18,130,1,128]{3,1,2,0:T(8,128)S(1)} collective-permute-done((f32[18,130,1,128]{3,1,2,0:T(8,128)S(1)}, f32[18,130,1,128]{3,1,2,0:T(8,128)S(1)}, u32[]{:S(2)}, u32[]{:S(2)}) %collective-permute-start.23) | collective-permute-done | bytes 1198112 | tf_op jit(solution)/shard_map/ppermute | solution.py:18
  407.7 25.3 %collective-permute-done.22 = f32[18,130,1,128]{3,1,2,0:T(8,128)S(1)} collective-permute-done((f32[18,130,1,128]{3,1,2,0:T(8,128)S(1)}, f32[18,130,1,128]{3,1,2,0:T(8,128)S(1)}, u32[]{:S(2)}, u32[]{:S(2)}) %collective-permute-start.22) | collective-permute-done | bytes 1198112 | tf_op jit(solution)/shard_map/ppermute | solution.py:15
  435.2 13.7 %fusion.4 = f32[16,128,8,128]{3,2,1,0:T(8,128)} fusion(f32[16,128,8,128]{3,2,1,0:T(8,128)} %param.7, f32[16,128,8,128]{3,2,1,0:T(8,128)S(1)} %copy-done.1, f32[16,128,8,128]{3,2,1,0:T(8,128)} %param.6, f32[18,130,1,128]{3,2,1,0:T(1,128)S(1)} %copy.39, f32[18,1,8,128]{3,2,1,0:T(8,128)S(1)} %collective-permute-done.21, ...), kind=kLoop, calls=%fused_computation.8 | loop fusion | flops 58720256 | bytes 37146624 | tf_op jit(solution)/shard_map/add | solution.py:52
  448.9 612.0 %reduce_window_sum.11 = f32[16,128,8,128]{3,2,1,0:T(8,128)} reduce-window(f32[16,128,8,128]{3,2,1,0:T(8,128)} %fusion.4, f32[]{:T(128)} %constant.34.clone.1), window={size=1x1x8x1 pad=0_0x0_0x7_0x0_0}, to_apply=%region_0.0 | reduce-window | flops 14680064 | bytes 16777220 | tf_op jit(solution)/shard_map/jit(cumsum)/reduce_window_sum | solution.py:59
  1066.5 78.7 %all-gather.3.cloned.1.call-done = f32[64,128,1,128]{3,1,2,0:T(8,128)} async-done(((f32[16,128,1,128]{3,1,2,0:T(8,128)}), f32[64,128,1,128]{3,1,2,0:T(8,128)}) %all-gather.3.cloned.1.call-update) | async-done | bytes 4194320 | tf_op jit(solution)/shard_map/all_gather | solution.py:25
  1145.2 9.2 while.14
  1154.4 7.8 add_multiply_fusion
  (91 shorter events, 88.5 us)
Async XLA Ops:
  7.2 1138.0 %all-gather.3.cloned.1.call-start = ((), (), s32[]{:S(2)}) async-start(), calls=%async_computation | async-start | bytes 5242880 | tf_op jit(solution)/shard_map/all_gather | solution.py:25
  8.5 14.9 %collective-permute-start = (f32[1,128,8,128]{3,2,1,0:T(8,128)S(1)}, f32[1,128,8,128]{3,2,1,0:T(8,128)S(1)}, u32[]{:S(2)}, u32[]{:S(2)}) collective-permute-start(f32[1,128,8,128]{3,2,1,0:T(8,128)S(1)} %get-tuple-element.142), channel_id=1, source_target_pairs={{0,16},{16,0},{1,17},{17,1},{2,18},{18,2},{3,19},{19,3},{4,20},{20... | collective-permute-start | bytes 1572872 | tf_op jit(solution)/shard_map/ppermute | solution.py:15
  10.1 23.4 %collective-permute-start.1 = (f32[1,128,8,128]{3,2,1,0:T(8,128)S(1)}, f32[1,128,8,128]{3,2,1,0:T(8,128)S(1)}, u32[]{:S(2)}, u32[]{:S(2)}) collective-permute-start(f32[1,128,8,128]{3,2,1,0:T(8,128)S(1)} %get-tuple-element.141), channel_id=1, source_target_pairs={{16,0},{0,16},{17,1},{1,17},{18,2},{2,18},{19,3},{3,19},{20,4},{4,... | collective-permute-start | bytes 1572872 | tf_op jit(solution)/shard_map/ppermute | solution.py:18
  33.5 3.8 collective-permute-start.2
  33.6 3.8 collective-permute-start.3
  39.3 31.7 %collective-permute-start.5 = (f32[18,130,1,128]{3,1,2,0:T(8,128)S(1)}, f32[18,130,1,128]{3,1,2,0:T(8,128)S(1)}, u32[]{:S(2)}, u32[]{:S(2)}) collective-permute-start(f32[18,130,1,128]{3,1,2,0:T(8,128)S(1)} %copy.26), channel_id=1, source_target_pairs={{1,0},{2,1},{3,2},{0,3},{5,4},{6,5},{7,6},{4,7},{9,8},{10,9},{11,1... | collective-permute-start | bytes 3594248 | tf_op jit(solution)/shard_map/ppermute | solution.py:18
  39.9 57.0 %collective-permute-start.4 = (f32[18,130,1,128]{3,1,2,0:T(8,128)S(1)}, f32[18,130,1,128]{3,1,2,0:T(8,128)S(1)}, u32[]{:S(2)}, u32[]{:S(2)}) collective-permute-start(f32[18,130,1,128]{3,1,2,0:T(8,128)S(1)} %copy.24), channel_id=1, source_target_pairs={{0,1},{1,2},{2,3},{3,0},{4,5},{5,6},{6,7},{7,4},{8,9},{9,10},{10,1... | collective-permute-start | bytes 3594248 | tf_op jit(solution)/shard_map/ppermute | solution.py:15
  125.1 14.9 %collective-permute-start.6 = (f32[1,128,8,128]{3,2,1,0:T(8,128)S(1)}, f32[1,128,8,128]{3,2,1,0:T(8,128)S(1)}, u32[]{:S(2)}, u32[]{:S(2)}) collective-permute-start(f32[1,128,8,128]{3,2,1,0:T(8,128)S(1)} %get-tuple-element.139), channel_id=1, source_target_pairs={{0,16},{16,0},{1,17},{17,1},{2,18},{18,2},{3,19},{19,3},{4,20},{20... | collective-permute-start | bytes 1572872 | tf_op jit(solution)/shard_map/ppermute | solution.py:15
  126.7 23.7 %collective-permute-start.7 = (f32[1,128,8,128]{3,2,1,0:T(8,128)S(1)}, f32[1,128,8,128]{3,2,1,0:T(8,128)S(1)}, u32[]{:S(2)}, u32[]{:S(2)}) collective-permute-start(f32[1,128,8,128]{3,2,1,0:T(8,128)S(1)} %get-tuple-element.140), channel_id=1, source_target_pairs={{16,0},{0,16},{17,1},{1,17},{18,2},{2,18},{19,3},{3,19},{20,4},{4,... | collective-permute-start | bytes 1572872 | tf_op jit(solution)/shard_map/ppermute | solution.py:18
  150.4 3.8 collective-permute-start.8
  150.5 3.8 collective-permute-start.9
  157.2 32.3 %collective-permute-start.11 = (f32[18,130,1,128]{3,1,2,0:T(8,128)S(1)}, f32[18,130,1,128]{3,1,2,0:T(8,128)S(1)}, u32[]{:S(2)}, u32[]{:S(2)}) collective-permute-start(f32[18,130,1,128]{3,1,2,0:T(8,128)S(1)} %copy.30), channel_id=1, source_target_pairs={{1,0},{2,1},{3,2},{0,3},{5,4},{6,5},{7,6},{4,7},{9,8},{10,9},{11,1... | collective-permute-start | bytes 3594248 | tf_op jit(solution)/shard_map/ppermute | solution.py:18
  157.8 57.3 %collective-permute-start.10 = (f32[18,130,1,128]{3,1,2,0:T(8,128)S(1)}, f32[18,130,1,128]{3,1,2,0:T(8,128)S(1)}, u32[]{:S(2)}, u32[]{:S(2)}) collective-permute-start(f32[18,130,1,128]{3,1,2,0:T(8,128)S(1)} %copy.28), channel_id=1, source_target_pairs={{0,1},{1,2},{2,3},{3,0},{4,5},{5,6},{6,7},{7,4},{8,9},{9,10},{10,1... | collective-permute-start | bytes 3594248 | tf_op jit(solution)/shard_map/ppermute | solution.py:15
  232.5 14.9 %collective-permute-start.12 = (f32[1,128,8,128]{3,2,1,0:T(8,128)S(1)}, f32[1,128,8,128]{3,2,1,0:T(8,128)S(1)}, u32[]{:S(2)}, u32[]{:S(2)}) collective-permute-start(f32[1,128,8,128]{3,2,1,0:T(8,128)S(1)} %get-tuple-element.137), channel_id=1, source_target_pairs={{0,16},{16,0},{1,17},{17,1},{2,18},{18,2},{3,19},{19,3},{4,20},{20... | collective-permute-start | bytes 1572872 | tf_op jit(solution)/shard_map/ppermute | solution.py:15
  234.1 23.7 %collective-permute-start.13 = (f32[1,128,8,128]{3,2,1,0:T(8,128)S(1)}, f32[1,128,8,128]{3,2,1,0:T(8,128)S(1)}, u32[]{:S(2)}, u32[]{:S(2)}) collective-permute-start(f32[1,128,8,128]{3,2,1,0:T(8,128)S(1)} %get-tuple-element.138), channel_id=1, source_target_pairs={{16,0},{0,16},{17,1},{1,17},{18,2},{2,18},{19,3},{3,19},{20,4},{4,... | collective-permute-start | bytes 1572872 | tf_op jit(solution)/shard_map/ppermute | solution.py:18
  258.7 3.8 collective-permute-start.14
  258.8 3.8 collective-permute-start.15
  265.5 32.1 %collective-permute-start.17 = (f32[18,130,1,128]{3,1,2,0:T(8,128)S(1)}, f32[18,130,1,128]{3,1,2,0:T(8,128)S(1)}, u32[]{:S(2)}, u32[]{:S(2)}) collective-permute-start(f32[18,130,1,128]{3,1,2,0:T(8,128)S(1)} %copy.34), channel_id=1, source_target_pairs={{1,0},{2,1},{3,2},{0,3},{5,4},{6,5},{7,6},{4,7},{9,8},{10,9},{11,1... | collective-permute-start | bytes 3594248 | tf_op jit(solution)/shard_map/ppermute | solution.py:18
  267.2 57.1 %collective-permute-start.16 = (f32[18,130,1,128]{3,1,2,0:T(8,128)S(1)}, f32[18,130,1,128]{3,1,2,0:T(8,128)S(1)}, u32[]{:S(2)}, u32[]{:S(2)}) collective-permute-start(f32[18,130,1,128]{3,1,2,0:T(8,128)S(1)} %copy.32), channel_id=1, source_target_pairs={{0,1},{1,2},{2,3},{3,0},{4,5},{5,6},{6,7},{7,4},{8,9},{9,10},{10,1... | collective-permute-start | bytes 3594248 | tf_op jit(solution)/shard_map/ppermute | solution.py:15
  341.7 14.9 %collective-permute-start.18 = (f32[1,128,8,128]{3,2,1,0:T(8,128)S(1)}, f32[1,128,8,128]{3,2,1,0:T(8,128)S(1)}, u32[]{:S(2)}, u32[]{:S(2)}) collective-permute-start(f32[1,128,8,128]{3,2,1,0:T(8,128)S(1)} %get-tuple-element.135), channel_id=1, source_target_pairs={{0,16},{16,0},{1,17},{17,1},{2,18},{18,2},{3,19},{19,3},{4,20},{20... | collective-permute-start | bytes 1572872 | tf_op jit(solution)/shard_map/ppermute | solution.py:15
  343.2 23.4 %collective-permute-start.19 = (f32[1,128,8,128]{3,2,1,0:T(8,128)S(1)}, f32[1,128,8,128]{3,2,1,0:T(8,128)S(1)}, u32[]{:S(2)}, u32[]{:S(2)}) collective-permute-start(f32[1,128,8,128]{3,2,1,0:T(8,128)S(1)} %get-tuple-element.136), channel_id=1, source_target_pairs={{16,0},{0,16},{17,1},{1,17},{18,2},{2,18},{19,3},{3,19},{20,4},{4,... | collective-permute-start | bytes 1572872 | tf_op jit(solution)/shard_map/ppermute | solution.py:18
  367.7 3.8 collective-permute-start.20
  374.5 32.0 %collective-permute-start.23 = (f32[18,130,1,128]{3,1,2,0:T(8,128)S(1)}, f32[18,130,1,128]{3,1,2,0:T(8,128)S(1)}, u32[]{:S(2)}, u32[]{:S(2)}) collective-permute-start(f32[18,130,1,128]{3,1,2,0:T(8,128)S(1)} %copy.38), channel_id=1, source_target_pairs={{1,0},{2,1},{3,2},{0,3},{5,4},{6,5},{7,6},{4,7},{9,8},{10,9},{11,1... | collective-permute-start | bytes 3594248 | tf_op jit(solution)/shard_map/ppermute | solution.py:18
  375.8 57.2 %collective-permute-start.22 = (f32[18,130,1,128]{3,1,2,0:T(8,128)S(1)}, f32[18,130,1,128]{3,1,2,0:T(8,128)S(1)}, u32[]{:S(2)}, u32[]{:S(2)}) collective-permute-start(f32[18,130,1,128]{3,1,2,0:T(8,128)S(1)} %copy.36), channel_id=1, source_target_pairs={{0,1},{1,2},{2,3},{3,0},{4,5},{5,6},{6,7},{7,4},{8,9},{9,10},{10,1... | collective-permute-start | bytes 3594248 | tf_op jit(solution)/shard_map/ppermute | solution.py:15
  (10 other events, 148.2 us)
Sparse Core Ops, SparseCore 0:
  1066.6 78.5 all-gather.2
where the time goes:
time: 1190 us; the launch traced here: 1170 us
  other arithmetic  705 us (59%)
  waiting for transfers between devices  386 us (32%)
  starting transfers between devices  31.5 us (3%)
  local copies, waits for them, and re-layouts  31.4 us (3%)
  between operations  14.8 us (1%)
    another operation x1, other arithmetic, on_device(): here = jnp.cumsum(tracer, axis=2)  612 us
    ppermute x12, waiting for transfers between devices, padded_2(): lax.ppermute(lax.slice_in_dim(block, block.shape[dim] - width, None, axis...  159 us
    ppermute x12, waiting for transfers between devices, padded_2(): lax.ppermute(lax.slice_in_dim(block, 0, width, axis=dim), axis, backward)  149 us
    all_gather x1, waiting for transfers between devices, entering(): pieces = lax.all_gather(value, axis)  78.7 us
    add x4, other arithmetic, one_step(): return middle + conductance * spread + source  68 us
  transfers between devices with their start and end apart: 25, of which 21 were waited for; matrix products, arithmetic and copies ran while one was open for 1% of the time, Pallas kernels for 0%

commit v1 on v0

v1 whole, which is shorter than its diff:
```python
import functools

import jax
import jax.numpy as jnp
from jax import lax
from jax.experimental import pallas as pl
from jax.experimental.pallas import tpu as pltpu
from jax.sharding import PartitionSpec as P

STEPS = 4
MESH = pl.DeviceIdType.MESH


def chunks_of(cells):
    for parts in (8, 4, 2):
        if cells % (8 * parts) == 0:
            return parts
    raise ValueError("x extent")


def evolve(
    counts, parts, deep, tracer, conductance, source, end, below,
    field, coeff, gain, zhalo, yhalo, xhalo, zface, entering, leaving,
    load_sem, zsend, zrecv, ysend, yrecv, xsend, xrecv, psend, precv, store_sem,
):
    rows_y, all_rows, members = tracer.shape
    cells = all_rows // deep
    wide = cells // parts
    rows = wide * deep
    count = dict(zip(("py", "px", "pz"), counts))
    mine = {axis: lax.axis_index(axis) for axis in count}
    after = {axis: lax.rem(mine[axis] + 1, count[axis]) for axis in count}
    before = {axis: lax.rem(mine[axis] + count[axis] - 1, count[axis]) for axis in count}
    body_y = pl.ds(1, rows_y)

    def span(c):
        return pl.ds(pl.multiple_of(c * rows, 8), rows)

    def inner(c):
        return pl.ds(pl.multiple_of(c * rows + deep, 8), rows)

    def cell_span(c):
        return pl.ds(pl.multiple_of(c * wide, 8), wide)

    def load(which, c):
        hbm, dst = (
            (tracer, field.at[0, body_y, inner(c), :]),
            (conductance, coeff.at[:, span(c), :]),
            (source, gain.at[:, span(c), :]),
        )[which]
        return pltpu.make_async_copy(hbm.at[:, span(c), :], dst, load_sem.at[which, c])

    def remote(src, dst, send, recv, axis, target):
        return pltpu.make_async_remote_copy(
            src_ref=src, dst_ref=dst, send_sem=send, recv_sem=recv,
            device_id={axis: target}, device_id_type=MESH,
        )

    def z_copy(t, side, c):
        return remote(
            zface.at[lax.rem(t, 2), side, :, cell_span(c), :],
            zhalo.at[t, side, :, cell_span(c), :],
            zsend.at[t, side, c], zrecv.at[t, side, c],
            "pz", (after, before)[side]["pz"],
        )

    def y_copy(t, side, c):
        return remote(
            field.at[lax.rem(t, 2), (rows_y, 1)[side], inner(c), :],
            yhalo.at[t, side, span(c), :],
            ysend.at[t, side, c], yrecv.at[t, side, c],
            "py", (after, before)[side]["py"],
        )

    def x_copy(t, side):
        return remote(
            field.at[lax.rem(t, 2), body_y, pl.ds((all_rows, deep)[side], deep), :],
            xhalo.at[t, side],
            xsend.at[t, side], xrecv.at[t, side],
            "px", (after, before)[side]["px"],
        )

    def prefix_copy(c):
        return remote(
            leaving.at[:, cell_span(c), :], entering.at[:, cell_span(c), :],
            psend.at[c], precv.at[c], "pz", after["pz"],
        )

    def store_end(c):
        return pltpu.make_async_copy(
            field.at[STEPS % 2, body_y, inner(c), :], end.at[:, span(c), :], store_sem.at[0, c]
        )

    def store_below(c):
        return pltpu.make_async_copy(
            entering.at[:, cell_span(c), :], below.at[:, cell_span(c), :], store_sem.at[1, c]
        )

    def send_faces(t, c):
        for side in (0, 1):
            z_copy(t, side, c).start()
            y_copy(t, side, c).start()

        @pl.when(c == 0)
        def _():
            x_copy(t, 1).start()

        @pl.when(c == parts - 1)
        def _():
            x_copy(t, 0).start()

    def face_of(p, y, c, z):
        return field[p, y, pl.ds(c * rows + deep + z, wide, stride=deep), :]

    def keep_z_faces(p, y, c):
        zface[p, 0, y, cell_span(c), :] = face_of(p, y + 1, c, deep - 1)
        zface[p, 1, y, cell_span(c), :] = face_of(p, y + 1, c, 0)

    def each_chunk(work):
        def run(c, carry):
            work(c)
            return carry

        lax.fori_loop(0, parts, run, 0)

    each_chunk(lambda c: load(0, c).start())

    def load_rest(c):
        load(1, c).start()
        load(2, c).start()

    each_chunk(load_rest)

    barrier = pltpu.get_barrier_semaphore()
    for axis in count:
        for target in (after[axis], before[axis]):
            pl.semaphore_signal(barrier, inc=1, device_id={axis: target}, device_id_type=MESH)
    pl.semaphore_wait(barrier, 6)

    def first_faces(c):
        load(0, c).wait()

        def row(y, carry):
            keep_z_faces(0, y, c)
            return carry

        lax.fori_loop(0, rows_y, row, 0)
        send_faces(0, c)

    each_chunk(first_faces)

    def wait_sent(t, c):
        for side in (0, 1):
            z_copy(t, side, c).wait_send()
            y_copy(t, side, c).wait_send()

        @pl.when(c == 0)
        def _():
            x_copy(t, 1).wait_send()

        @pl.when(c == parts - 1)
        def _():
            x_copy(t, 0).wait_send()

    level = lax.broadcasted_iota(jnp.int32, (wide, deep, members), 1)

    def step(t, carry):
        old, new = lax.rem(t, 2), lax.rem(t + 1, 2)

        def chunk(c):
            @pl.when(t == 0)
            def _():
                load(1, c).wait()
                load(2, c).wait()

            @pl.when(t > 0)
            def _():
                wait_sent(t - 1, c)

            for side in (0, 1):
                z_copy(t, side, c).wait_recv()
                y_copy(t, side, c).wait_recv()
                field[old, (0, rows_y + 1)[side], inner(c), :] = yhalo[t, side, span(c), :]

            @pl.when(c == 0)
            def _():
                x_copy(t, 0).wait_recv()
                field[old, body_y, pl.ds(0, deep), :] = xhalo[t, 0]

            @pl.when(c == parts - 1)
            def _():
                x_copy(t, 1).wait_recv()
                field[old, body_y, pl.ds(all_rows + deep, deep), :] = xhalo[t, 1]

            def row(y, carry):
                def at(dy, dx):
                    start = pl.multiple_of(c * rows + deep + dx * deep, 8)
                    return field[old, y + 1 + dy, pl.ds(start, rows), :]

                def tall(values):
                    return jnp.broadcast_to(values[:, None, :], (wide, deep, members))

                middle = at(0, 0)
                block = middle.reshape(wide, deep, members)
                first = tall(zhalo[t, 0, y, cell_span(c), :])
                last = tall(zhalo[t, 1, y, cell_span(c), :])
                lower = jnp.where(level == 0, first, pltpu.roll(block, 1, 1))
                upper = jnp.where(level == deep - 1, last, pltpu.roll(block, deep - 1, 1))
                along = (lower + upper).reshape(rows, members)
                spread = at(-1, 0) + at(1, 0) + at(0, -1) + at(0, 1) + along - 6.0 * middle
                field[new, y + 1, inner(c), :] = (
                    middle + coeff[y, span(c), :] * spread + gain[y, span(c), :]
                )
                return carry

            lax.fori_loop(0, rows_y, row, 0)

            @pl.when(t < STEPS - 1)
            def _():
                def faces(y, carry):
                    keep_z_faces(new, y, c)
                    return carry

                lax.fori_loop(0, rows_y, faces, 0)
                send_faces(t + 1, c)

            @pl.when(t == STEPS - 1)
            def _():
                store_end(c).start()

                def totals(y, carry):
                    total = face_of(new, y + 1, c, 0)
                    for z in range(1, deep):
                        total = total + face_of(new, y + 1, c, z)
                    leaving[y, cell_span(c), :] = total
                    return carry

                lax.fori_loop(0, rows_y, totals, 0)

                @pl.when(mine["pz"] == 0)
                def _():
                    entering[:, cell_span(c), :] = jnp.zeros((rows_y, wide, members), jnp.float32)

                @pl.when(mine["pz"] > 0)
                def _():
                    prefix_copy(c).wait_recv()
                    leaving[:, cell_span(c), :] += entering[:, cell_span(c), :]

                @pl.when(mine["pz"] < count["pz"] - 1)
                def _():
                    prefix_copy(c).start()

                store_below(c).start()

        each_chunk(chunk)
        return carry

    lax.fori_loop(0, STEPS, step, 0)

    def finish(c):
        wait_sent(STEPS - 1, c)
        store_end(c).wait()
        store_below(c).wait()

        @pl.when(mine["pz"] < count["pz"] - 1)
        def _():
            prefix_copy(c).wait_send()

    each_chunk(finish)


def sums(depth, end, below, potential, tracer_end):
    _, all_rows, members = end.shape
    cells = below.shape[1]
    deep = all_rows // cells
    values = end[0]
    tracer_end[0] = values
    block = values.reshape(cells, deep, members)
    level = lax.broadcasted_iota(jnp.int32, block.shape, 1)
    reach = 1
    while reach < deep:
        block = block + jnp.where(level >= reach, pltpu.roll(block, reach, 1), 0.0)
        reach *= 2
    block = block + jnp.broadcast_to(below[0][:, None, :], block.shape)
    potential[0] = (block / depth).reshape(all_rows, members)


def on_device(counts, tracer, conductance, source):
    shape = tracer.shape
    rows_y, cells, deep, members = shape
    parts = chunks_of(cells)
    rows = cells * deep
    flat = (rows_y, rows, members)
    anywhere = pl.BlockSpec(memory_space=pl.ANY)
    f32 = jnp.float32
    dma = pltpu.SemaphoreType.DMA
    end, below = pl.pallas_call(
        functools.partial(evolve, counts, parts, deep),
        out_shape=(
            jax.ShapeDtypeStruct(flat, f32),
            jax.ShapeDtypeStruct((rows_y, cells, members), f32),
        ),
        in_specs=[anywhere] * 3,
        out_specs=(anywhere, anywhere),
        scratch_shapes=[
            pltpu.VMEM((2, rows_y + 2, rows + 2 * deep, members), f32),
            pltpu.VMEM(flat, f32),
            pltpu.VMEM(flat, f32),
            pltpu.VMEM((STEPS, 2, rows_y, cells, members), f32),
            pltpu.VMEM((STEPS, 2, rows, members), f32),
            pltpu.VMEM((STEPS, 2, rows_y, deep, members), f32),
            pltpu.VMEM((2, 2, rows_y, cells, members), f32),
            pltpu.VMEM((rows_y, cells, members), f32),
            pltpu.VMEM((rows_y, cells, members), f32),
            dma((3, parts)),
            dma((STEPS, 2, parts)), dma((STEPS, 2, parts)),
            dma((STEPS, 2, parts)), dma((STEPS, 2, parts)),
            dma((STEPS, 2)), dma((STEPS, 2)),
            dma((parts,)), dma((parts,)),
            dma((2, parts)),
        ],
        compiler_params=pltpu.CompilerParams(
            collective_id=0, has_side_effects=True, vmem_limit_bytes=64 * 1000 * 1000
        ),
        name="evolve",
    )(*(array.reshape(flat) for array in (tracer, conductance, source)))
    tall = pl.BlockSpec((1, rows, members), lambda y: (y, 0, 0))
    potential, tracer_end = pl.pallas_call(
        functools.partial(sums, deep * counts[2]),
        grid=(rows_y,),
        out_shape=(jax.ShapeDtypeStruct(flat, f32),) * 2,
        in_specs=[tall, pl.BlockSpec((1, cells, members), lambda y: (y, 0, 0))],
        out_specs=(tall, tall),
        name="sums",
    )(end, below)
    return potential.reshape(shape), tracer_end.reshape(shape)


def solution(mesh):
    placed = P("py", "px", "pz", None)
    counts = tuple(mesh.shape[axis] for axis in ("py", "px", "pz"))
    return jax.shard_map(
        functools.partial(on_device, counts),
        mesh=mesh,
        in_specs=(placed,) * 3,
        out_specs=(placed,) * 2,
        check_vma=False,
    )
```

time: 1190 us -> 235 us (0.20); the launches traced: 1170 us -> 235 us
  other arithmetic: 705 us -> 0 us
  waiting for transfers between devices: 386 us -> 0 us
  Pallas kernels: 0 us -> 234 us
  starting transfers between devices: 31.5 us -> 0 us
  local copies, waits for them, and re-layouts: 31.4 us -> 0 us
  between operations: 14.8 us -> 0.64 us
    another operation x1 -> x0, other arithmetic: 612 us -> none  [on_device(): here = jnp.cumsum(tracer, axis=2)]
    ppermute x24 -> x0, waiting for transfers between devices: 308 us -> none  [the longest x12 159 us: padded_2(): lax.ppermute(lax.slice_in_dim(block, block.shape[dim] - width, None, axis...]
    pallas_call x0 -> x2, Pallas kernels: none -> 234 us  [the longest x1 219 us: on_device(): pl.pallas_call(functools.partial(evolve, counts, parts, deep), out_shape=...]
    all_gather x1 -> x0, waiting for transfers between devices: 78.7 us -> none  [entering(): pieces = lax.all_gather(value, axis)]
    add x4 -> x0, other arithmetic: 68 us -> none  [one_step(): return middle + conductance * spread + source]
    ppermute x24 -> x0, starting transfers between devices: 31.4 us -> none  [the longest x12 18.7 us: padded_2(): lax.ppermute(lax.slice_in_dim(block, block.shape[dim] - width, None, axis...]
    ppermute x8 -> x0, local copies, waits for them, and re-layouts: 12.9 us -> none  [the longest x4 7.99 us: padded_2(): lax.ppermute(lax.slice_in_dim(block, block.shape[dim] - width, None, axis...]
    slice x7 -> x0, other arithmetic: 12.4 us -> none  [padded_2(): lax.slice_in_dim(block, block.shape[dim] - width, None, axis=dim)]
  transfers between devices with their start and end apart: 25 -> 0, of which waited for: 21 -> 0; matrix products, arithmetic and copies ran while one was open for 1% -> 0% of each run, Pallas kernels for 0% -> 0%
where the time goes in v1:
time: 235 us
  Pallas kernels  234 us (100%)
    pallas_call x1, Pallas kernels, on_device(): pl.pallas_call(functools.partial(evolve, counts, parts, deep), out_shape=...  219 us
    pallas_call x1, Pallas kernels, on_device(): pl.pallas_call(functools.partial(sums, deep * counts[2]), grid=(rows_y,),...  14.5 us

profile of v1, /device:TPU:24, one launch (start us, length us, event | category | flops | bytes accessed | tf_op | source)
XLA Modules:
  0.0 234.6 jit_solution(13042414013046475544)
XLA Ops:
  0.6 219.4 %evolve.1 = (f32[16,1024,128]{2,1,0:T(8,128)}, f32[16,128,128]{2,1,0:T(8,128)}) custom-call(f32[16,1024,128]{2,1,0:T(8,128)} %bitcast.5, f32[16,1024,128]{2,1,0:T(8,128)} %bitcast.6, f32[16,1024,128]{2,1,0:T(8,128)} %bitcast.7), custom_call_target="tpu_custom_call" | custom-call | tf_op jit(solution)/shard_map/evolve/pallas_call | solution.py:297
  220.0 14.5 %sums.1 = (f32[16,1024,128]{2,1,0:T(8,128)}, f32[16,1024,128]{2,1,0:T(8,128)}) custom-call(f32[16,1024,128]{2,1,0:T(8,128)} %get-tuple-element.6.end, f32[16,128,128]{2,1,0:T(8,128)} %get-tuple-element.7.below), custom_call_target="tpu_custom_call" | custom-call | tf_op jit(solution)/shard_map/sums/pallas_call | solution.py:328

commit v2 on v1

--- a/solution.py
+++ b/solution.py
@@ -21,12 +21,13 @@
 def evolve(
     counts, parts, deep, tracer, conductance, source, end, below,
     field, coeff, gain, zhalo, yhalo, xhalo, zface, entering, leaving,
-    load_sem, zsend, zrecv, ysend, yrecv, xsend, xrecv, psend, precv, store_sem,
+    load_sem, zsend, zrecv, ysend, yrecv, xsend, xrecv, psend, precv,
 ):
     rows_y, all_rows, members = tracer.shape
     cells = all_rows // deep
     wide = cells // parts
     rows = wide * deep
+    halves = psend.shape[1]
     count = dict(zip(("py", "px", "pz"), counts))
     mine = {axis: lax.axis_index(axis) for axis in count}
     after = {axis: lax.rem(mine[axis] + 1, count[axis]) for axis in count}
@@ -80,20 +81,13 @@
             "px", (after, before)[side]["px"],
         )
 
-    def prefix_copy(c):
+    def part_y(h):
+        return pl.ds(h * (rows_y // halves), rows_y // halves)
+
+    def prefix_copy(c, h):
         return remote(
-            leaving.at[:, cell_span(c), :], entering.at[:, cell_span(c), :],
-            psend.at[c], precv.at[c], "pz", after["pz"],
-        )
-
-    def store_end(c):
-        return pltpu.make_async_copy(
-            field.at[STEPS % 2, body_y, inner(c), :], end.at[:, span(c), :], store_sem.at[0, c]
-        )
-
-    def store_below(c):
-        return pltpu.make_async_copy(
-            entering.at[:, cell_span(c), :], below.at[:, cell_span(c), :], store_sem.at[1, c]
+            leaving.at[part_y(h), cell_span(c), :], entering.at[part_y(h), cell_span(c), :],
+            psend.at[c, h], precv.at[c, h], "pz", after["pz"],
         )
 
     def send_faces(t, c):
@@ -123,13 +117,8 @@
 
         lax.fori_loop(0, parts, run, 0)
 
-    each_chunk(lambda c: load(0, c).start())
-
-    def load_rest(c):
-        load(1, c).start()
-        load(2, c).start()
-
-    each_chunk(load_rest)
+    load(0, 0).start()
+    load(0, 1).start()
 
     barrier = pltpu.get_barrier_semaphore()
     for axis in count:
@@ -140,12 +129,18 @@
     def first_faces(c):
         load(0, c).wait()
 
+        @pl.when(c < parts - 2)
+        def _():
+            load(0, c + 2).start()
+
         def row(y, carry):
             keep_z_faces(0, y, c)
             return carry
 
         lax.fori_loop(0, rows_y, row, 0)
         send_faces(0, c)
+        load(1, c).start()
+        load(2, c).start()
 
     each_chunk(first_faces)
 
@@ -226,9 +221,8 @@
 
             @pl.when(t == STEPS - 1)
             def _():
-                store_end(c).start()
-
                 def totals(y, carry):
+                    end[y, span(c), :] = field[new, y + 1, inner(c), :]
                     total = face_of(new, y + 1, c, 0)
                     for z in range(1, deep):
                         total = total + face_of(new, y + 1, c, z)
@@ -240,49 +234,80 @@
                 @pl.when(mine["pz"] == 0)
                 def _():
                     entering[:, cell_span(c), :] = jnp.zeros((rows_y, wide, members), jnp.float32)
-
-                @pl.when(mine["pz"] > 0)
-                def _():
-                    prefix_copy(c).wait_recv()
-                    leaving[:, cell_span(c), :] += entering[:, cell_span(c), :]
+                    for h in range(halves):
+                        prefix_copy(c, h).start()
+
+        each_chunk(chunk)
+        return carry
+
+    lax.fori_loop(0, STEPS, step, 0)
+
+    @pl.when(mine["pz"] > 0)
+    def _():
+        def pass_on(c):
+            for h in range(halves):
+                prefix_copy(c, h).wait_recv()
 
                 @pl.when(mine["pz"] < count["pz"] - 1)
                 def _():
-                    prefix_copy(c).start()
-
-                store_below(c).start()
-
-        each_chunk(chunk)
+                    leaving[part_y(h), cell_span(c), :] += entering[part_y(h), cell_span(c), :]
+                    prefix_copy(c, h).start()
+
+        each_chunk(pass_on)
+
+    def keep_below(y, carry):
+        below[y] = entering[y]
         return carry
 
-    lax.fori_loop(0, STEPS, step, 0)
+    lax.fori_loop(0, rows_y, keep_below, 0)
 
     def finish(c):
         wait_sent(STEPS - 1, c)
-        store_end(c).wait()
-        store_below(c).wait()
 
         @pl.when(mine["pz"] < count["pz"] - 1)
         def _():
-            prefix_copy(c).wait_send()
+            for h in range(halves):
+                prefix_copy(c, h).wait_send()
 
     each_chunk(finish)
 
 
-def sums(depth, end, below, potential, tracer_end):
-    _, all_rows, members = end.shape
+def sums(depth, end, below, potential, tracer_end, ready, end_sem, sum_sem):
+    rows_y, all_rows, members = end.shape
     cells = below.shape[1]
     deep = all_rows // cells
-    values = end[0]
-    tracer_end[0] = values
-    block = values.reshape(cells, deep, members)
-    level = lax.broadcasted_iota(jnp.int32, block.shape, 1)
-    reach = 1
-    while reach < deep:
-        block = block + jnp.where(level >= reach, pltpu.roll(block, reach, 1), 0.0)
-        reach *= 2
-    block = block + jnp.broadcast_to(below[0][:, None, :], block.shape)
-    potential[0] = (block / depth).reshape(all_rows, members)
+    slots = ready.shape[0]
+    level = lax.broadcasted_iota(jnp.int32, (cells, deep, members), 1)
+    whole = pltpu.make_async_copy(end, tracer_end, end_sem)
+    whole.start()
+
+    def store(y):
+        slot = lax.rem(y, slots)
+        return pltpu.make_async_copy(ready.at[slot], potential.at[y], sum_sem.at[slot])
+
+    def row(y, carry):
+        @pl.when(y >= slots)
+        def _():
+            store(y - slots).wait()
+
+        block = end[y].reshape(cells, deep, members)
+        reach = 1
+        while reach < deep:
+            block = block + jnp.where(level >= reach, pltpu.roll(block, reach, 1), 0.0)
+            reach *= 2
+        block = block + jnp.broadcast_to(below[y][:, None, :], block.shape)
+        ready[lax.rem(y, slots)] = (block / depth).reshape(all_rows, members)
+        store(y).start()
+        return carry
+
+    lax.fori_loop(0, rows_y, row, 0)
+
+    def drain(y, carry):
+        store(y).wait()
+        return carry
+
+    lax.fori_loop(rows_y - slots, rows_y, drain, 0)
+    whole.wait()
 
 
 def on_device(counts, tracer, conductance, source):
@@ -290,18 +315,20 @@
     rows_y, cells, deep, members = shape
     parts = chunks_of(cells)
     rows = cells * deep
+    halves = 2 if rows_y % 2 == 0 else 1
     flat = (rows_y, rows, members)
     anywhere = pl.BlockSpec(memory_space=pl.ANY)
+    near = pl.BlockSpec(memory_space=pltpu.VMEM)
     f32 = jnp.float32
     dma = pltpu.SemaphoreType.DMA
     end, below = pl.pallas_call(
         functools.partial(evolve, counts, parts, deep),
         out_shape=(
-            jax.ShapeDtypeStruct(flat, f32),
-            jax.ShapeDtypeStruct((rows_y, cells, members), f32),
+            pltpu.VMEM(flat, f32),
+            pltpu.VMEM((rows_y, cells, members), f32),
         ),
         in_specs=[anywhere] * 3,
-        out_specs=(anywhere, anywhere),
+        out_specs=(near, near),
         scratch_shapes=[
             pltpu.VMEM((2, rows_y + 2, rows + 2 * deep, members), f32),
             pltpu.VMEM(flat, f32),
@@ -316,21 +343,21 @@
             dma((STEPS, 2, parts)), dma((STEPS, 2, parts)),
             dma((STEPS, 2, parts)), dma((STEPS, 2, parts)),
             dma((STEPS, 2)), dma((STEPS, 2)),
-            dma((parts,)), dma((parts,)),
-            dma((2, parts)),
+            dma((parts, halves)), dma((parts, halves)),
         ],
         compiler_params=pltpu.CompilerParams(
-            collective_id=0, has_side_effects=True, vmem_limit_bytes=64 * 1000 * 1000
+            collective_id=0, has_side_effects=True, vmem_limit_bytes=53 * 1024 * 1024 + 524288
         ),
         name="evolve",
     )(*(array.reshape(flat) for array in (tracer, conductance, source)))
-    tall = pl.BlockSpec((1, rows, members), lambda y: (y, 0, 0))
+    slots = min(4, rows_y)
     potential, tracer_end = pl.pallas_call(
         functools.partial(sums, deep * counts[2]),
-        grid=(rows_y,),
         out_shape=(jax.ShapeDtypeStruct(flat, f32),) * 2,
-        in_specs=[tall, pl.BlockSpec((1, cells, members), lambda y: (y, 0, 0))],
-        out_specs=(tall, tall),
+        in_specs=[near, near],
+        out_specs=(anywhere, anywhere),
+        scratch_shapes=[pltpu.VMEM((slots, rows, members), f32), dma(()), dma((slots,))],
+        compiler_params=pltpu.CompilerParams(vmem_limit_bytes=16 * 1024 * 1024),
         name="sums",
     )(end, below)
     return potential.reshape(shape), tracer_end.reshape(shape)

time: 235 us -> 224 us (0.953)
  Pallas kernels: 234 us -> 223 us
    pallas_call x1, Pallas kernels: 14.5 us -> 7.4 us  [on_device(): pl.pallas_call(functools.partial(sums, deep * counts[2]), out_shape=(jax....]
    pallas_call x1, Pallas kernels: 219 us -> 216 us  [on_device(): pl.pallas_call(functools.partial(evolve, counts, parts, deep), out_shape=...]
where the time goes in v2:
time: 224 us
  Pallas kernels  223 us (100%)
    pallas_call x1, Pallas kernels, on_device(): pl.pallas_call(functools.partial(evolve, counts, parts, deep), out_shape=...  216 us
    pallas_call x1, Pallas kernels, on_device(): pl.pallas_call(functools.partial(sums, deep * counts[2]), out_shape=(jax....  7.4 us

profile of v2, /device:TPU:24, one launch (start us, length us, event | category | flops | bytes accessed | tf_op | source)
XLA Modules:
  0.0 224.0 jit_solution(856642731732926784)
XLA Ops:
  0.6 216.0 %evolve.1 = (f32[16,1024,128]{2,1,0:T(8,128)S(1)}, f32[16,128,128]{2,1,0:T(8,128)S(1)}) custom-call(f32[16,1024,128]{2,1,0:T(8,128)} %bitcast.5, f32[16,1024,128]{2,1,0:T(8,128)} %bitcast.6, f32[16,1024,128]{2,1,0:T(8,128)} %bitcast.7), custom_call_target="tpu_custom_call" | custom-call | tf_op jit(solution)/shard_map/evolve/pallas_call | solution.py:324
  216.6 7.4 %sums.1 = (f32[16,1024,128]{2,1,0:T(8,128)}, f32[16,1024,128]{2,1,0:T(8,128)}) custom-call(f32[16,1024,128]{2,1,0:T(8,128)S(1)} %get-tuple-element.6.end, f32[16,128,128]{2,1,0:T(8,128)S(1)} %get-tuple-element.7.below), custom_call_target="tpu_custom_call" | custom-call | tf_op jit(solution)/shard_map/sums/pallas_call | solution.py:354

commit v3 on v2

--- a/solution.py
+++ b/solution.py
@@ -315,7 +315,7 @@
     rows_y, cells, deep, members = shape
     parts = chunks_of(cells)
     rows = cells * deep
-    halves = 2 if rows_y % 2 == 0 else 1
+    halves = next((h for h in (4, 2) if rows_y % h == 0), 1)
     flat = (rows_y, rows, members)
     anywhere = pl.BlockSpec(memory_space=pl.ANY)
     near = pl.BlockSpec(memory_space=pltpu.VMEM)

time: 224 us -> 223 us (level)
  no operation moved by 1% of the time
where the time goes in v3:
time: 223 us
  Pallas kernels  223 us (100%)
    pallas_call x1, Pallas kernels, on_device(): pl.pallas_call(functools.partial(evolve, counts, parts, deep), out_shape=...  215 us
    pallas_call x1, Pallas kernels, on_device(): pl.pallas_call(functools.partial(sums, deep * counts[2]), out_shape=(jax....  7.4 us

profile of v3, /device:TPU:24, one launch (start us, length us, event | category | flops | bytes accessed | tf_op | source)
XLA Modules:
  0.0 223.2 jit_solution(1581654713909067731)
XLA Ops:
  0.6 215.1 %evolve.1 = (f32[16,1024,128]{2,1,0:T(8,128)S(1)}, f32[16,128,128]{2,1,0:T(8,128)S(1)}) custom-call(f32[16,1024,128]{2,1,0:T(8,128)} %bitcast.5, f32[16,1024,128]{2,1,0:T(8,128)} %bitcast.6, f32[16,1024,128]{2,1,0:T(8,128)} %bitcast.7), custom_call_target="tpu_custom_call" | custom-call | tf_op jit(solution)/shard_map/evolve/pallas_call | solution.py:324
  215.8 7.4 %sums.1 = (f32[16,1024,128]{2,1,0:T(8,128)}, f32[16,1024,128]{2,1,0:T(8,128)}) custom-call(f32[16,1024,128]{2,1,0:T(8,128)S(1)} %get-tuple-element.6.end, f32[16,128,128]{2,1,0:T(8,128)S(1)} %get-tuple-element.7.below), custom_call_target="tpu_custom_call" | custom-call | tf_op jit(solution)/shard_map/sums/pallas_call | solution.py:354
